TPU v7x, 32 devices: a whole 2x2x4 slice. The times are simulated.
32 devices in a mesh: grid: 8 (over y, x, core), rows: 4 (over z).
Axes of the slice: x: 2, y: 2, z: 4, core: 2. Of those that a mesh axis runs over, the one named last changes fastest.
Arguments:
- density: bfloat16 [32, 128, 4096], P(None, 'rows', 'grid'), as said below
- basis_values: bfloat16 [16, 16, 128, 512], P('grid', None, 'rows'), may hold values from -0.59765625 to 0.59765625
- grid_points: float32 [16, 3, 512], P('grid'), may hold values from -4 to 4
- grid_weights: float32 [16, 512], P('grid'), may hold values from 0.05 to 1
- screened_blocks: int32 [16, 16], P('grid'), may hold values from 0 to 31, as said below
Outputs:
- exchange: float32 [32, 128, 4096], P(None, 'rows', 'grid')
Inputs may be any that keep to these rules, and one draw needn't show every extreme that they name: density is symmetric: density[a, i, b * 128 + j] equals density[b, j, a * 128 + i]. `screened_blocks`: each row holds 16 distinct block numbers.
All inputs are finite; a program needn't handle non-finite values.
Results may differ from a plain program's by a relative error of at most 0.00055.
The roundings to bfloat16 on the way count: a program that leaves them out, or rounds other values in their place, can miss the bound.
Values may be sent and summed in bfloat16 or wider, within the bound.
A program may use at most 128 MiB of HBM per device.

v0:
```python
import jax
import jax.numpy as jnp
from jax import lax
from jax.sharding import PartitionSpec as P


def body(density, basis_values, grid_points, grid_weights, screened_blocks):
    nblocks = density.shape[0]
    rows_mine = density.shape[1]
    block_size = rows_mine * lax.axis_size("rows")
    nbasis = nblocks * block_size
    nsig = basis_values.shape[1]
    npoints = basis_values.shape[3]
    stripe = lax.all_gather(density, "grid", axis=2, tiled=True)
    totals = jnp.zeros((nblocks, rows_mine, nblocks, block_size), jnp.float32)
    for batch_index in range(basis_values.shape[0]):
        blocks = screened_blocks[batch_index]
        row_pick = jnp.take(stripe, blocks, axis=0).reshape(nsig * rows_mine, nblocks, block_size)
        chosen = jnp.take(row_pick, blocks, axis=1)
        local_values = basis_values[batch_index]
        x_mine = local_values.reshape(nsig * rows_mine, npoints)
        fsum = jnp.einsum(
            "mtk,tkp->mp",
            chosen,
            lax.all_gather(local_values, "rows", axis=1, tiled=True),
            preferred_element_type=jnp.float32,
        )
        fmat = fsum.astype(jnp.bfloat16)
        intersection_part = lax.dot_general(
            x_mine, fmat, (((0,), (0,)), ((), ())), preferred_element_type=jnp.float32
        )
        intersection = lax.psum(intersection_part, "rows")
        places = grid_points[batch_index]
        weights = grid_weights[batch_index]
        diffs = places[:, :, None] - places[:, None, :]
        kern = 1.0 / jnp.sqrt(jnp.sum(diffs * diffs, axis=0) + 0.5)
        mixed = (weights[:, None] * kern * intersection).astype(jnp.bfloat16)
        potential = (
            jnp.dot(x_mine, mixed, preferred_element_type=jnp.float32) * weights[None, :]
        ).astype(jnp.bfloat16)
        potential = potential.reshape(nsig, rows_mine, npoints)
        block_k = jnp.einsum(
            "mp,tkp->mtk",
            x_mine,
            lax.all_gather(potential, "rows", axis=1, tiled=True),
            preferred_element_type=jnp.float32,
        )
        block_k = block_k.reshape(nsig, rows_mine, nsig, block_size)
        totals = totals.at[blocks[:, None], :, blocks[None, :], :].add(
            block_k.transpose(0, 2, 1, 3)
        )
    return lax.psum_scatter(
        totals.reshape(nblocks, rows_mine, nbasis), "grid", scatter_dimension=2, tiled=True
    )


def solution(mesh):
    placed = (
        P(None, "rows", "grid"),
        P("grid", None, "rows", None),
        P("grid", None, None),
        P("grid", None),
        P("grid", None),
    )
    return jax.shard_map(
        body, mesh=mesh, in_specs=placed, out_specs=P(None, "rows", "grid"), check_vma=False
    )
```

profile of v0, /device:TPU:2, one launch (start us, length us, event | category | flops | bytes accessed | tf_op | source)
XLA Modules:
  0.0 571.0 jit_solution(16403228100501752769)
XLA Ops:
  7.3 2.3 fusion.56
  10.5 55.8 %all-gather.8.cloned.1.call-done = bf16[32,32,4096]{2,1,0:T(8,128)(2,1)} async-done(((bf16[32,32,512]{2,1,0:T(8,128)(2,1)}), bf16[32,32,4096]{2,1,0:T(8,128)(2,1)}) %all-gather.8.cloned.1.call-update) | async-done | bytes 8388624 | tf_op jit(solution)/shard_map/all_gather | solution.py:14
  66.3 6.2 %gather_fusion.2 = bf16[16,32,4096]{2,1,0:T(8,128)(2,1)} fusion(bf16[32,32,4096]{2,1,0:T(8,128)(2,1)} %all-gather.8.cloned.1.call-done, s32[1024]{0:T(1024)S(1)} %pad_clamp_fusion), kind=kCustom, calls=%fused_computation.2.clone | custom fusion | bytes 8388672 | tf_op jit(solution)/shard_map/jit(_take)/gather | solution.py:18
  72.5 2.7 broadcast_select_fusion
  75.2 1.3 copy.31
  76.4 3.6 copy.23
  80.0 3.1 gather_fusion.3
  83.2 6.2 %gather_fusion = bf16[16,32,4096]{2,1,0:T(8,128)(2,1)} fusion(bf16[32,32,4096]{2,1,0:T(8,128)(2,1)} %all-gather.8.cloned.1.call-done, s32[1024]{0:T(1024)S(1)} %pad_clamp_fusion.1), kind=kCustom, calls=%fused_computation.clone | custom fusion | bytes 8388672 | tf_op jit(solution)/shard_map/jit(_take)/gather | solution.py:18
  89.4 2.7 broadcast_select_fusion.1
  92.1 1.3 copy.30
  93.3 3.6 copy.19
  96.9 4.4 gather_fusion.1
  101.3 12.2 %all-gather.16.cloned.1.call-done = bf16[1,16,128,512]{3,2,1,0:T(8,128)(2,1)} async-done(((bf16[1,16,32,512]{3,2,1,0:T(8,128)(2,1)}), bf16[1,16,128,512]{3,2,1,0:T(8,128)(2,1)}) %all-gather.16.cloned.1.call-update) | async-done | bytes 2097168 | tf_op jit(solution)/shard_map/all_gather | solution.py:25
  113.6 4.3 convolution_bitcast_fusion.2
  117.9 41.8 %all-gather.14.cloned.1.call-done = bf16[1,16,128,512]{3,2,1,0:T(8,128)(2,1)} async-done(((bf16[1,16,32,512]{3,2,1,0:T(8,128)(2,1)}), bf16[1,16,128,512]{3,2,1,0:T(8,128)(2,1)}) %all-gather.14.cloned.1.call-update) | async-done | bytes 2097168 | tf_op jit(solution)/shard_map/all_gather | solution.py:25
  159.7 4.9 convolution_bitcast_fusion.3
  165.4 84.3 %all-reduce.3.cloned.1.call-done = (f32[512,512]{0,1:T(8,128)}, f32[512,512]{0,1:T(8,128)}) async-done(((f32[512,512]{0,1:T(8,128)}, f32[512,512]{0,1:T(8,128)}), (f32[512,512]{0,1:T(8,128)}, f32[512,512]{0,1:T(8,128)})) %all-reduce.3.cloned.1.call-update) | async-done | bytes 2097168 | tf_op jit(solution)/shard_map/psum | solution.py:32
  249.7 2.5 fusion.20
  253.0 2.5 fusion.21
  256.1 41.0 %all-gather.10.cloned.1.call-done = bf16[16,128,512]{2,1,0:T(8,128)(2,1)} async-done(((bf16[16,32,512]{2,1,0:T(8,128)(2,1)}), bf16[16,128,512]{2,1,0:T(8,128)(2,1)}) %all-gather.10.cloned.1.call-update) | async-done | bytes 2097168 | tf_op jit(solution)/shard_map/all_gather | solution.py:45
  297.1 4.8 convolution_bitcast_fusion.1
  301.9 5.6 copy.20
  307.5 5.5 copy.21
  312.9 30.1 %all-gather.12.cloned.1.call-done = bf16[16,128,512]{2,1,0:T(8,128)(2,1)} async-done(((bf16[16,32,512]{2,1,0:T(8,128)(2,1)}), bf16[16,128,512]{2,1,0:T(8,128)(2,1)}) %all-gather.12.cloned.1.call-update) | async-done | bytes 2097168 | tf_op jit(solution)/shard_map/all_gather | solution.py:45
  343.0 4.8 convolution_bitcast_fusion
  347.8 5.5 copy.24
  353.3 5.5 copy.25
  358.8 7.9 %broadcast_in_dim.45 = f32[32,32,32,128]{3,1,2,0:T(8,128)} broadcast(f32[]{:T(128)} %constant.20.clone.1), dimensions={} | broadcast | bytes 16777220 | tf_op jit(solution)/shard_map/broadcast_in_dim | solution.py:15
  366.7 35.4 %scatter_fusion = f32[32,32,32,128]{3,1,2,0:T(8,128)} fusion(f32[32,32,32,128]{3,1,2,0:T(8,128)} %broadcast_in_dim.45, s32[256]{0:T(256)S(1)} %reshape.132, f32[256,32,128]{2,1,0:T(8,128)} %bitcast.123), kind=kCustom, calls=%fused_computation.4 | custom fusion | flops 1048576 | bytes 12584960 | tf_op jit(solution)/shard_map/scatter-add | solution.py:49
  402.1 35.4 %scatter_fusion.1 = f32[32,32,32,128]{3,1,2,0:T(8,128)} fusion(f32[32,32,32,128]{3,1,2,0:T(8,128)} %scatter_fusion, s32[256]{0:T(256)S(1)} %reshape.138, f32[256,32,128]{2,1,0:T(8,128)} %bitcast.124), kind=kCustom, calls=%fused_computation.5 | custom fusion | flops 1048576 | bytes 12584960 | tf_op jit(solution)/shard_map/scatter-add | solution.py:49
  437.5 11.7 %copy_bitcast_fusion = f32[32,32,4096]{2,1,0:T(8,128)} fusion(f32[32,32,32,128]{3,1,2,0:T(8,128)} %scatter_fusion.1), kind=kLoop, calls=%fused_computation.6 | loop fusion | bytes 33554432 | tf_op jit(solution)/shard_map/reshape | solution.py:53
  449.2 115.0 %reduce-scatter.2.cloned.1.call-done = f32[32,32,512]{2,1,0:T(8,128)} async-done(((f32[32,32,4096]{2,1,0:T(8,128)}), f32[32,32,512]{2,1,0:T(8,128)}) %reduce-scatter.2.cloned.1.call-update) | async-done | bytes 2097168 | tf_op jit(solution)/shard_map/reduce_scatter | solution.py:52
  (42 shorter events, 3.6 us)
Async XLA Ops:
  6.5 3.9 copy-start.4
  6.5 59.8 %all-gather.8.cloned.1.call-start = ((), (), s32[]{:S(2)}) async-start(), calls=%async_computation.1 | async-start | bytes 9437184 | tf_op jit(solution)/shard_map/all_gather | solution.py:14
  7.3 106.3 %all-gather.16.cloned.1.call-start = ((), (), s32[]{:S(2)}) async-start(), calls=%async_computation.6 | async-start | bytes 2621440 | tf_op jit(solution)/shard_map/all_gather | solution.py:25
  9.6 150.0 %all-gather.14.cloned.1.call-start = ((), (), s32[]{:S(2)}) async-start(), calls=%async_computation.5 | async-start | bytes 2621440 | tf_op jit(solution)/shard_map/all_gather | solution.py:25
  10.4 239.3 %all-reduce.3.cloned.1.call-start = ((), (), s32[]{:S(2)}) async-start(), calls=%async_computation.7 | async-start | bytes 4194304 | tf_op jit(solution)/shard_map/psum | solution.py:32
  96.9 16.7 %copy-start = (bf16[1,16,32,512]{3,2,1,0:T(8,128)(2,1)S(1)}, bf16[1,16,32,512]{3,2,1,0:T(8,128)(2,1)}, u32[]{:S(2)}) copy-start(bf16[1,16,32,512]{3,2,1,0:T(8,128)(2,1)} %get-tuple-element.13) | copy-start | bytes 1572868
  113.6 46.1 %copy-start.1 = (bf16[1,16,32,512]{3,2,1,0:T(8,128)(2,1)S(1)}, bf16[1,16,32,512]{3,2,1,0:T(8,128)(2,1)}, u32[]{:S(2)}) copy-start(bf16[1,16,32,512]{3,2,1,0:T(8,128)(2,1)} %get-tuple-element.14) | copy-start | bytes 1572868
  159.7 5.0 copy-start.2
  164.5 0.8 copy-start.3
  164.6 132.5 %all-gather.10.cloned.1.call-start = ((), (), s32[]{:S(2)}) async-start(), calls=%async_computation.2 | async-start | bytes 2621440 | tf_op jit(solution)/shard_map/all_gather | solution.py:45
  252.2 90.8 %all-gather.12.cloned.1.call-start = ((), (), s32[]{:S(2)}) async-start(), calls=%async_computation.3 | async-start | bytes 2621440 | tf_op jit(solution)/shard_map/all_gather | solution.py:45
  255.5 308.6 %reduce-scatter.2.cloned.1.call-start = ((), (), s32[]{:S(2)}) async-start(), calls=%async_computation.4 | async-start | bytes 18874368 | tf_op jit(solution)/shard_map/reduce_scatter | solution.py:52
Sparse Core Ops, SparseCore 0:
  9.2 57.0 all-gather.7
  67.9 45.6 all-gather.15
  115.2 44.4 all-gather.13
  164.7 84.9 all-reduce.2
  252.4 44.6 all-gather.9
  298.5 44.4 all-gather.11
  449.3 114.8 reduce-scatter.1
where the time goes:
time: 574 us; the launch traced here: 571 us
  waiting for transfers between devices  382 us (67%)
  other arithmetic  76.9 us (13%)
  local copies, waits for them, and re-layouts  74.4 us (13%)
  matrix products  23.9 us (4%)
  between operations  13.7 us (2%)
    reduce_scatter x1, waiting for transfers between devices, body(): lax.psum_scatter(totals.reshape(nblocks, rows_mine, nbasis), 'grid', scat...  115 us
    psum x1, waiting for transfers between devices, body(): intersection = lax.psum(intersection_part, 'rows')  84.3 us
    all_gather x2, waiting for transfers between devices, body(): lax.all_gather(potential, 'rows', axis=1, tiled=True)  71.1 us
    scatter-add x2, other arithmetic, body(): totals.at[blocks[:, None], :, blocks[None, :], :]  70.7 us
    all_gather x1, waiting for transfers between devices, body(): stripe = lax.all_gather(density, 'grid', axis=2, tiled=True)  55.8 us
    all_gather x2, waiting for transfers between devices, body(): lax.all_gather(local_values, 'rows', axis=1, tiled=True)  54 us
    gather x2, local copies, waits for them, and re-layouts, body(): jnp.take(stripe, blocks, axis=0)  12.4 us
    reshape x1, local copies, waits for them, and re-layouts, body(): totals.reshape(nblocks, rows_mine, nbasis)  11.7 us
  transfers between devices with their start and end apart: 7, of which 7 were waited for; matrix products, arithmetic and copies ran while one was open for 11% of the time, Pallas kernels for 0%

commit v1 on v0

v1 whole, which is shorter than its diff:
```python
import functools

import jax
import jax.numpy as jnp
from jax import lax
from jax.experimental import pallas as pl
from jax.experimental.pallas import tpu as pltpu
from jax.sharding import PartitionSpec as P

MESH = pl.DeviceIdType.MESH
F32 = jnp.float32
BF16 = jnp.bfloat16
CORES = 2
GROUP = 128
LEVELS = 32767.0
TINY = 2.0 ** -110


def kernel(
    ngrid, nrows, sel_ref, part_ref, cut_ref, inv_ref, p_ref, x_ref, pts_ref, ptst_ref, w_ref, wt_ref, out_ref,
    p_all, x_all, psel, fm_send, fm_all, mixed, xpad, pot, lhs, rhs, pair_send, pair_recv,
    q_send, q_recv, s_send, s_recv,
    p_out, p_pair, p_in, x_up, x_down, x_in, local, fm_out, fm_in, m_up, m_down, m_in,
    pair_out, pair_in, q_out, q_in, s_out, s_in,
):
    me = lax.axis_index("grid")
    z = lax.axis_index("rows")
    core = lax.rem(me, CORES)
    chip = me // CORES
    nchip = ngrid // CORES
    partner = chip * CORES + (CORES - 1 - core)
    nblk, bpd, rows, bs = p_ref.shape
    nb, nsig, _, npts = x_ref.shape
    cols = bpd * bs
    split = nrows // nb
    half = npts // split

    def peer(k):
        return lax.rem(chip + k, nchip) * CORES + core

    def origin(k):
        return lax.rem(chip + nchip - k, nchip) * CORES + core

    barrier = pltpu.get_barrier_semaphore()
    for k in range(1, nrows):
        pl.semaphore_signal(barrier, inc=1, device_id=(me, lax.rem(z + k, nrows)), device_id_type=MESH)
    for k in range(1, nchip):
        pl.semaphore_signal(barrier, inc=1, device_id=(peer(k), z), device_id_type=MESH)
    pl.semaphore_signal(barrier, inc=1, device_id=(partner, z), device_id_type=MESH)
    pl.semaphore_wait(barrier, nrows - 1 + nchip - 1 + 1)

    def remote(src, dst, send, recv, device):
        return pltpu.make_async_remote_copy(
            src_ref=src, dst_ref=dst, send_sem=send, recv_sem=recv, device_id=device, device_id_type=MESH
        )

    def x_slot(batch, owner):
        return x_all.at[batch, :, pl.ds(pl.multiple_of(owner * rows, rows), rows), :]

    def x_copy(batch, owner, step, src=None):
        up = step > 0
        sems = x_up if up else x_down
        return remote(
            x_slot(batch, owner) if src is None else src, x_slot(batch, owner),
            sems.at[batch, owner], x_in.at[batch, owner], (me, z + step),
        )

    for batch in range(nb):
        mine = x_ref.at[batch]

        @pl.when(z > 0)
        def _():
            x_copy(batch, z, -1, mine).start()

        @pl.when(z < nrows - 1)
        def _():
            x_copy(batch, z, 1, mine).start()

    def p_copy(k):
        return remote(p_ref, p_all.at[me], p_out.at[k], p_in.at[me], (peer(k), z))

    def p_wait(k):
        return remote(p_ref, p_all.at[origin(k)], p_out.at[k], p_in.at[origin(k)], (peer(k), z))

    def p_forward(k):
        src = p_ref if k == 0 else p_all.at[origin(k)]
        return remote(src, p_all.at[origin(k)], p_pair.at[k], p_in.at[origin(k)], (partner, z))

    def p_pair_wait(k):
        slot = lax.rem(chip + nchip - k, nchip) * CORES + (CORES - 1 - core)
        return remote(p_ref, p_all.at[slot], p_pair.at[k], p_in.at[slot], (partner, z))

    for k in range(1, nchip):
        p_copy(k).start()
    p_forward(0).start()

    locals_ = [pltpu.make_async_copy(p_ref, p_all.at[me], local.at[0])]
    for batch in range(nb):
        locals_.append(pltpu.make_async_copy(x_ref.at[batch], x_slot(batch, z), local.at[1 + batch]))
        locals_.append(
            pltpu.make_async_copy(x_ref.at[batch], xpad.at[batch, pl.ds(0, nsig)], local.at[1 + nb + batch])
        )
    for copy in locals_:
        copy.start()
    for batch in range(nb):
        xpad[batch, nsig] = jnp.zeros((rows, npts), BF16)
        pot[batch, nsig] = jnp.zeros((bs, npts), BF16)
    for copy in locals_:
        copy.wait()

    for batch in range(nb):
        def fill(block, carry):
            lhs[pl.ds(pl.multiple_of(block * rows, rows), rows), batch * npts:(batch + 1) * npts] = xpad[
                batch, inv_ref[batch, block]
            ]
            return carry
        lax.fori_loop(0, nblk, fill, 0)

    def x_arrive(dist, batch):
        @pl.when(z + dist < nrows)
        def _():
            x_copy(batch, z + dist, -1).wait_recv()

            @pl.when(z > 0)
            def _():
                x_copy(batch, z + dist, -1).start()

        @pl.when(z - dist >= 0)
        def _():
            x_copy(batch, z - dist, 1).wait_recv()

            @pl.when(z < nrows - 1)
            def _():
                x_copy(batch, z - dist, 1).start()

    for dist in range(1, nrows - 1):
        for batch in range(nb):
            x_arrive(dist, batch)
    for k in range(1, nchip):
        p_wait(k).wait_recv()
        p_forward(k).start()
    for k in range(nchip):
        p_pair_wait(k).wait_recv()

    def fm_slot(owner):
        return fm_all.at[:, pl.ds(pl.multiple_of(owner * rows, rows), rows), :]

    def fm_copy(owner):
        return remote(fm_send.at[owner], fm_slot(z), fm_out.at[owner], fm_in.at[z], (me, owner))

    def fm_wait(source):
        return remote(fm_send.at[0], fm_slot(source), fm_out.at[0], fm_in.at[source], (me, source))

    for batch in range(nb):
        x_arrive(nrows - 1, batch)

        def pick(s, carry):
            row = sel_ref[batch, s]
            for t in range(nsig):
                psel[pl.ds(pl.multiple_of(s * rows, rows), rows), t * bs:(t + 1) * bs] = p_all[
                    part_ref[batch, t], row, cut_ref[batch, t]
                ]
            return carry
        lax.fori_loop(0, nsig, pick, 0)
        for h in range(split):
            got = jnp.dot(
                psel[...], x_all[batch, :, :, h * half:(h + 1) * half].reshape(nsig * bs, half),
                preferred_element_type=F32,
            )
            fm_send[batch * split + h] = got.astype(BF16).reshape(nsig, rows, half)
        for h in range(split):
            owner = batch * split + h

            @pl.when(z != owner)
            def _():
                fm_copy(owner).start()

            @pl.when(z == owner)
            def _():
                own = pltpu.make_async_copy(fm_send.at[owner], fm_slot(z), local.at[0])
                own.start()
                own.wait()

    for source in range(nrows):
        @pl.when(z != source)
        def _():
            fm_wait(source).wait_recv()

    bmine = z // split
    hmine = lax.rem(z, split)
    lanes = pl.ds(pl.multiple_of(hmine * half, half), half)
    tile = npts // 4
    for piece in range(4):
        q = slice(piece * tile, (piece + 1) * tile)
        inter = lax.dot_general(
            x_all[bmine, :, :, q].reshape(nsig * bs, tile), fm_all[...].reshape(nsig * bs, half),
            (((0,), (0,)), ((), ())), preferred_element_type=F32,
        )
        dist2 = None
        for axis in range(3):
            diff = ptst_ref[bmine, q, axis:axis + 1] - pts_ref[bmine, axis:axis + 1, lanes]
            dist2 = diff * diff if dist2 is None else dist2 + diff * diff
        kern = 1.0 / jnp.sqrt(dist2 + 0.5)
        mixed[z, q, :] = (wt_ref[bmine, q, :] * kern * inter).astype(BF16)

    def m_copy(owner, step):
        sems = m_up if step > 0 else m_down
        return remote(mixed.at[owner], mixed.at[owner], sems.at[owner], m_in.at[owner], (me, z + step))

    @pl.when(z > 0)
    def _():
        m_copy(z, -1).start()

    @pl.when(z < nrows - 1)
    def _():
        m_copy(z, 1).start()

    for dist in range(1, nrows):
        @pl.when(z + dist < nrows)
        def _():
            m_copy(z + dist, -1).wait_recv()

            @pl.when(z > 0)
            def _():
                m_copy(z + dist, -1).start()

        @pl.when(z - dist >= 0)
        def _():
            m_copy(z - dist, 1).wait_recv()

            @pl.when(z < nrows - 1)
            def _():
                m_copy(z - dist, 1).start()

    for batch in range(nb):
        for h in range(split):
            cut = slice(h * half, (h + 1) * half)

            def fill_pot(part, carry):
                some = pl.ds(part * 4, 4)
                got = jnp.dot(
                    x_all[batch, some].reshape(4 * bs, npts), mixed[batch * split + h], preferred_element_type=F32
                ) * w_ref[batch, :, cut]
                pot[batch, some, :, cut] = got.astype(BF16).reshape(4, bs, half)
                return carry
            lax.fori_loop(0, nsig // 4, fill_pot, 0)

    total_rows = nblk * rows
    step_rows = 2 * GROUP
    steps = total_rows // step_rows

    def fill_rhs(dest):
        for t in range(bpd):
            for batch in range(nb):
                rhs[t * bs:(t + 1) * bs, batch * npts:(batch + 1) * npts] = pot[
                    batch, inv_ref[batch, dest * bpd + t]
                ]

    def product(at):
        return lax.dot_general(
            lhs[pl.ds(at, step_rows), :], rhs[...], (((1,), (1,)), ((), ())), preferred_element_type=F32
        )

    def pair_copy(k):
        return remote(pair_send.at[k], pair_recv.at[k], pair_out.at[k], pair_in.at[k], (partner, z))

    def q_copy(k):
        return remote(q_send.at[k], q_recv.at[k], q_out.at[k], q_in.at[k], (peer(k), z))

    def s_copy(k):
        return remote(s_send.at[k], s_recv.at[k], s_out.at[k], s_in.at[k], (peer(k), z))

    for k in list(range(1, nchip)) + [0]:
        fill_rhs(lax.rem(chip + k, nchip) * CORES + (CORES - 1 - core))

        def theirs(i, carry):
            at = pl.multiple_of(i * step_rows, step_rows)
            pair_send[k, pl.ds(at, step_rows), :] = product(at)
            return carry
        lax.fori_loop(0, steps, theirs, 0)
        pair_copy(k).start()
        fill_rhs(lax.rem(chip + k, nchip) * CORES + core)
        pair_copy(k).wait_recv()

        def ours(i, carry):
            at = pl.multiple_of(i * step_rows, step_rows)
            value = product(at) + pair_recv[k, pl.ds(at, step_rows), :]
            if k == 0:
                out_ref[pl.ds(at, step_rows), :] = value
                return carry
            for g in range(2):
                some = value[g * GROUP:(g + 1) * GROUP]
                top = jnp.maximum(jnp.max(jnp.abs(some), axis=0, keepdims=True), TINY)
                s_send[k, i * 2 + g] = jnp.broadcast_to(top * (1.0 / LEVELS), (8, cols))
                q_send[k, pl.ds(pl.multiple_of(at + g * GROUP, GROUP), GROUP), :] = (
                    jnp.round(some * (LEVELS / top)).astype(jnp.int32).astype(jnp.int16)
                )
            return carry
        lax.fori_loop(0, steps, ours, 0)
        if k > 0:
            q_copy(k).start()
            s_copy(k).start()

    for k in range(1, nchip):
        q_copy(k).wait_recv()
        s_copy(k).wait_recv()

        def add(i, carry):
            at = pl.ds(pl.multiple_of(i * GROUP, GROUP), GROUP)
            out_ref[at, :] = out_ref[at, :] + q_recv[k, at, :].astype(jnp.int32).astype(F32) * s_recv[k, i, 0:1, :]
            return carry
        lax.fori_loop(0, total_rows // GROUP, add, 0)

    for k in range(nchip):
        p_forward(k).wait_send()
        pair_copy(k).wait_send()
        if k > 0:
            p_copy(k).wait_send()
            q_copy(k).wait_send()
            s_copy(k).wait_send()
    for owner in range(nrows):
        @pl.when(z != owner)
        def _():
            fm_copy(owner).wait_send()

        @pl.when(jnp.logical_and(z > 0, owner >= z))
        def _():
            for batch in range(nb):
                x_copy(batch, owner, -1).wait_send()
            m_copy(owner, -1).wait_send()

        @pl.when(jnp.logical_and(z < nrows - 1, owner <= z))
        def _():
            for batch in range(nb):
                x_copy(batch, owner, 1).wait_send()
            m_copy(owner, 1).wait_send()


def body(ngrid, nrows, density, basis_values, grid_points, grid_weights, screened_blocks):
    nblk, rows, cols = density.shape
    nb, nsig, _, npts = basis_values.shape
    bs = rows * nrows
    nchip = ngrid // CORES
    half = npts // (nrows // nb)
    total_rows = nblk * rows
    hit = screened_blocks[:, None, :] == jnp.arange(nblk, dtype=jnp.int32)[None, :, None]
    slot = jnp.arange(nsig, dtype=jnp.int32)
    inverse = jnp.min(jnp.where(hit, slot, nsig), axis=2).astype(jnp.int32)
    vmem = pl.BlockSpec(memory_space=pltpu.VMEM)
    smem = pl.BlockSpec(memory_space=pltpu.SMEM)
    dma = pltpu.SemaphoreType.DMA
    out = pl.pallas_call(
        functools.partial(kernel, ngrid, nrows),
        out_shape=jax.ShapeDtypeStruct((total_rows, cols), F32),
        in_specs=[smem] * 4 + [vmem] * 6,
        out_specs=vmem,
        scratch_shapes=[
            pltpu.VMEM((ngrid, nblk, cols // bs, rows, bs), BF16),
            pltpu.VMEM((nb, nsig, bs, npts), BF16),
            pltpu.VMEM((nsig * rows, nsig * bs), BF16),
            pltpu.VMEM((nrows, nsig, rows, half), BF16),
            pltpu.VMEM((nsig, bs, half), BF16),
            pltpu.VMEM((nrows, npts, half), BF16),
            pltpu.VMEM((nb, nsig + 1, rows, npts), BF16),
            pltpu.VMEM((nb, nsig + 1, bs, npts), BF16),
            pltpu.VMEM((total_rows, nb * npts), BF16),
            pltpu.VMEM((cols, nb * npts), BF16),
            pltpu.VMEM((nchip, total_rows, cols), F32),
            pltpu.VMEM((nchip, total_rows, cols), F32),
            pltpu.VMEM((nchip, total_rows, cols), jnp.int16),
            pltpu.VMEM((nchip, total_rows, cols), jnp.int16),
            pltpu.VMEM((nchip, total_rows // GROUP, 8, cols), F32),
            pltpu.VMEM((nchip, total_rows // GROUP, 8, cols), F32),
            dma((nchip,)), dma((nchip,)), dma((ngrid,)),
            dma((nb, nrows)), dma((nb, nrows)), dma((nb, nrows)),
            dma((1 + 2 * nb,)),
            dma((nrows,)), dma((nrows,)),
            dma((nrows,)), dma((nrows,)), dma((nrows,)),
            dma((nchip,)), dma((nchip,)), dma((nchip,)), dma((nchip,)), dma((nchip,)), dma((nchip,)),
        ],
        compiler_params=pltpu.CompilerParams(
            collective_id=0, has_side_effects=True, vmem_limit_bytes=63 * 1024 * 1024
        ),
        name="exchange",
    )(
        screened_blocks, screened_blocks // (cols // bs), screened_blocks % (cols // bs), inverse,
        density.reshape(nblk, rows, cols // bs, bs).swapaxes(1, 2), basis_values, grid_points, jnp.swapaxes(grid_points, 1, 2),
        grid_weights[:, None, :], grid_weights[:, :, None],
    )
    return out.reshape(nblk, rows, cols)


def solution(mesh):
    placed = (
        P(None, "rows", "grid"),
        P("grid", None, "rows", None),
        P("grid", None, None),
        P("grid", None),
        P("grid", None),
    )
    return jax.shard_map(
        functools.partial(body, mesh.shape["grid"], mesh.shape["rows"]), mesh=mesh, in_specs=placed,
        out_specs=P(None, "rows", "grid"), check_vma=False,
    )
```

time: 574 us -> 208 us (0.36)
  waiting for transfers between devices: 382 us -> 0 us
  Pallas kernels: 0 us -> 193 us
  other arithmetic: 76.9 us -> 2.64 us
  local copies, waits for them, and re-layouts: 74.4 us -> 11.6 us
  matrix products: 23.9 us -> 0 us
  between operations: 13.7 us -> 0.01 us
    pallas_call x0 -> x1, Pallas kernels: none -> 193 us  [body(): pl.pallas_call(functools.partial(kernel, ngrid, nrows), out_shape=jax.Sha...]
    all_gather x5 -> x0, waiting for transfers between devices: 181 us -> none  [the longest x2 71.1 us: body(): lax.all_gather(potential, 'rows', axis=1, tiled=True)]
    reduce_scatter x1 -> x0, waiting for transfers between devices: 115 us -> none  [body(): lax.psum_scatter(totals.reshape(nblocks, rows_mine, nbasis), 'grid', scat...]
    psum x1 -> x0, waiting for transfers between devices: 84.3 us -> none  [body(): intersection = lax.psum(intersection_part, 'rows')]
    scatter-add x2 -> x0, other arithmetic: 70.7 us -> none  [body(): totals.at[blocks[:, None], :, blocks[None, :], :]]
    dot_general x6 -> x0, matrix products: 23.9 us -> none  [the longest x2 9.67 us: body(): jnp.einsum('mp,tkp->mtk', x_mine, lax.all_gather(potential, 'rows', axis=...]
    gather x4 -> x0, local copies, waits for them, and re-layouts: 19.9 us -> none  [the longest x2 12.4 us: body(): jnp.take(stripe, blocks, axis=0)]
    reshape x3 -> x0, local copies, waits for them, and re-layouts: 18.9 us -> none  [the longest x1 11.7 us: body(): totals.reshape(nblocks, rows_mine, nbasis)]
  transfers between devices with their start and end apart: 7 -> 0, of which waited for: 7 -> 0; matrix products, arithmetic and copies ran while one was open for 11% -> 0% of each run, Pallas kernels for 0% -> 0%
where the time goes in v1:
time: 208 us; the launch traced here: 207 us
  Pallas kernels  193 us (93%)
  local copies, waits for them, and re-layouts  11.6 us (6%)
  other arithmetic  2.64 us (1%)
    pallas_call x1, Pallas kernels, body(): pl.pallas_call(functools.partial(kernel, ngrid, nrows), out_shape=jax.Sha...  193 us
    unnamed x3, local copies, waits for them, and re-layouts  6.22 us

profile of v1, /device:TPU:2, one launch (start us, length us, event | category | flops | bytes accessed | tf_op | source)
XLA Modules:
  0.0 207.4 jit_solution(335076752706706775)
XLA Ops:
  0.0 1.4 select_reduce_fusion.inv_ref
  1.4 1.3 and_select_fusion
  2.6 1.3 broadcast_in_dim.18.w_ref
  3.9 1.3 copy.14.pts_ref
  5.2 1.7 copy.15.wt_ref
  6.9 1.7 copy.13
  8.7 2.4 %bitcast_bitcast_fusion.p_ref = bf16[32,4,32,128]{3,2,1,0:T(8,128)(2,1)} fusion(bf16[32,32,512]{2,1,0:T(8,128)(2,1)} %param.5), kind=kLoop, calls=%fused_computation | loop fusion | bytes 2097152 | tf_op jit(solution)/shard_map/transpose | solution.py:387
  11.1 193.1 %exchange.1 = f32[1024,512]{1,0:T(8,128)} custom-call(s32[2,16]{1,0:T(2,128)} %sel_ref.1, s32[2,16]{1,0:T(2,128)} %get-tuple-element.6.part_ref, s32[2,16]{1,0:T(2,128)} %get-tuple-element.5.cut_ref, s32[2,32]{1,0:T(2,128)} %select_reduce_fusion.inv_ref, bf16[32,4,32,128]{3,2,1,0:T(8,128)(2,1)} %bitcast_bitcast_fusion.p_ref, bf16[2,16,32,512]{3,2,1,0:T(8,128)(2,1)} %x_ref.1, ...), custom_call_target="tpu_custom_call" | custom-call | tf_op jit(solution)/shard_map/exchange/pallas_call | solution.py:352
  204.2 3.2 %copy.19 = f32[32,32,512]{2,1,0:T(8,128)} copy(f32[32,32,512]{2,1,0:T(8,128)} %bitcast.10) | data formatting | bytes 4194304

commit v2 on v1

v2 whole, which is shorter than its diff:
```python
import functools

import jax
import jax.numpy as jnp
from jax import lax
from jax.experimental import pallas as pl
from jax.experimental.pallas import tpu as pltpu
from jax.sharding import PartitionSpec as P

MESH = pl.DeviceIdType.MESH
F32 = jnp.float32
BF16 = jnp.bfloat16
CORES = 2
GROUP = 128
LEVELS = 32767.0
TINY = 2.0 ** -110


def kernel(
    ngrid, nrows, sel_ref, inv_ref, p_ref, x_ref, pts_ref, w_ref, out_ref,
    p_mine, p_all, x_all, psel, fm_send, fm_all, mixed, xpad, pot, lhs, rhs, pair_send, pair_recv,
    q_send, q_recv, s_send, s_recv,
    p_out, p_pair, p_in, x_up, x_down, x_in, local, fm_out, fm_in, m_up, m_down, m_in,
    pair_out, pair_in, q_out, q_in, s_out, s_in,
):
    me = lax.axis_index("grid")
    z = lax.axis_index("rows")
    core = lax.rem(me, CORES)
    chip = me // CORES
    nchip = ngrid // CORES
    square = nchip == 4
    partner = chip * CORES + (CORES - 1 - core)
    nblk, rows, cols = p_ref.shape
    nb, nsig, _, npts = x_ref.shape
    bs = rows * nrows
    bpd = cols // bs
    split = nrows // nb
    half = npts // split
    pieces = 2
    part = nsig // pieces

    def toward(k):
        if square:
            return chip + (k % 2) * (1 - 2 * lax.rem(chip, 2)) + (k // 2) * (2 - 4 * (chip // 2))
        return lax.rem(chip + k, nchip)

    def source(k):
        return toward(k) if square else lax.rem(chip + nchip - k, nchip)

    def peer(k):
        return toward(k) * CORES + core

    def origin(k):
        return source(k) * CORES + core

    barrier = pltpu.get_barrier_semaphore()
    for k in range(1, nrows):
        pl.semaphore_signal(barrier, inc=1, device_id=(me, lax.rem(z + k, nrows)), device_id_type=MESH)
    for k in range(1, nchip):
        pl.semaphore_signal(barrier, inc=1, device_id=(peer(k), z), device_id_type=MESH)
    pl.semaphore_signal(barrier, inc=1, device_id=(partner, z), device_id_type=MESH)
    for t in range(bpd):
        p_mine[t] = p_ref[:, :, t * bs:(t + 1) * bs]
    pl.semaphore_wait(barrier, nrows - 1 + nchip - 1 + 1)

    def remote(src, dst, send, recv, device):
        return pltpu.make_async_remote_copy(
            src_ref=src, dst_ref=dst, send_sem=send, recv_sem=recv, device_id=device, device_id_type=MESH
        )

    def x_slot(batch, owner, c):
        return x_all.at[batch, pl.ds(c * part, part), pl.ds(pl.multiple_of(owner * rows, rows), rows), :]

    def x_copy(batch, owner, c, step, own=False):
        sems = x_up if step > 0 else x_down
        src = x_ref.at[batch, pl.ds(c * part, part)] if own else x_slot(batch, owner, c)
        return remote(
            src, x_slot(batch, owner, c), sems.at[batch, owner, c], x_in.at[batch, owner, c], (me, z + step)
        )

    def x_begin(batch):
        for c in range(pieces):
            @pl.when(z > 0)
            def _():
                x_copy(batch, z, c, -1, True).start()

            @pl.when(z < nrows - 1)
            def _():
                x_copy(batch, z, c, 1, True).start()

    def x_arrive(batch, dist):
        for c in range(pieces):
            @pl.when(z + dist < nrows)
            def _():
                x_copy(batch, z + dist, c, -1).wait_recv()

                @pl.when(z > 0)
                def _():
                    x_copy(batch, z + dist, c, -1).start()

            @pl.when(z - dist >= 0)
            def _():
                x_copy(batch, z - dist, c, 1).wait_recv()

                @pl.when(z < nrows - 1)
                def _():
                    x_copy(batch, z - dist, c, 1).start()

    def p_slot(owner):
        return p_all.at[pl.ds(owner * bpd, bpd)]

    def p_copy(k):
        return remote(p_mine, p_slot(me), p_out.at[k], p_in.at[me], (peer(k), z))

    def p_wait(k):
        return remote(p_mine, p_slot(origin(k)), p_out.at[k], p_in.at[origin(k)], (peer(k), z))

    def p_forward(k):
        src = p_mine if k == 0 else p_slot(origin(k))
        return remote(src, p_slot(origin(k)), p_pair.at[k], p_in.at[origin(k)], (partner, z))

    def p_pair_wait(k):
        slot = source(k) * CORES + (CORES - 1 - core)
        return remote(p_mine, p_slot(slot), p_pair.at[k], p_in.at[slot], (partner, z))

    x_begin(0)
    for k in range(1, nchip):
        p_copy(k).start()
    p_forward(0).start()

    locals_ = [pltpu.make_async_copy(p_mine, p_slot(me), local.at[0])]
    for batch in range(nb):
        for c in range(pieces):
            locals_.append(pltpu.make_async_copy(
                x_ref.at[batch, pl.ds(c * part, part)], x_slot(batch, z, c), local.at[1 + batch * pieces + c]
            ))
        locals_.append(pltpu.make_async_copy(
            x_ref.at[batch], xpad.at[batch, pl.ds(0, nsig)], local.at[1 + nb * pieces + batch]
        ))
    for copy in locals_:
        copy.start()
    for batch in range(nb):
        xpad[batch, nsig] = jnp.zeros((rows, npts), BF16)
        pot[batch, nsig] = jnp.zeros((bs, npts), BF16)
    for copy in locals_:
        copy.wait()

    for batch in range(nb):
        def fill(block, carry):
            lhs[pl.ds(pl.multiple_of(block * rows, rows), rows), batch * npts:(batch + 1) * npts] = xpad[
                batch, inv_ref[batch, block]
            ]
            return carry
        lax.fori_loop(0, nblk, fill, 0)

    def fm_slot(batch, owner):
        return fm_all.at[:, pl.ds(pl.multiple_of(owner * rows, rows), rows), :]

    def fm_copy(owner):
        return remote(fm_send.at[owner], fm_slot(0, z), fm_out.at[owner], fm_in.at[z], (me, owner))

    def fm_wait(other):
        return remote(fm_send.at[0], fm_slot(0, other), fm_out.at[0], fm_in.at[other], (me, other))

    def products(batch):
        def pick(s, carry):
            for t in range(nsig):
                psel[pl.ds(pl.multiple_of(s * rows, rows), rows), t * bs:(t + 1) * bs] = p_all[
                    sel_ref[batch, t], sel_ref[batch, s]
                ]
            return carry
        lax.fori_loop(0, nsig, pick, 0)
        for h in range(split):
            owner = batch * split + h
            got = jnp.dot(
                psel[...], x_all[batch, :, :, h * half:(h + 1) * half].reshape(nsig * bs, half),
                preferred_element_type=F32,
            )
            fm_send[owner] = got.astype(BF16).reshape(nsig, rows, half)
        for h in range(split):
            owner = batch * split + h

            @pl.when(z != owner)
            def _():
                fm_copy(owner).start()

            @pl.when(z == owner)
            def _():
                own = pltpu.make_async_copy(fm_send.at[owner], fm_slot(0, z), local.at[0])
                own.start()
                own.wait()

    def m_copy(owner, step):
        sems = m_up if step > 0 else m_down
        return remote(mixed.at[owner], mixed.at[owner], sems.at[owner], m_in.at[owner], (me, z + step))

    def mix(batch):
        @pl.when(z // split == batch)
        def _():
            for other in range(nrows):
                @pl.when(z != other)
                def _():
                    fm_wait(other).wait_recv()
            lanes = pl.ds(pl.multiple_of(lax.rem(z, split) * half, half), half)
            flipped = jnp.concatenate(
                [pts_ref[batch], w_ref[batch:batch + 1, :], jnp.zeros((4, npts), F32)], axis=0
            ).T
            tile = npts // 2
            for piece in range(2):
                q = slice(piece * tile, (piece + 1) * tile)
                inter = lax.dot_general(
                    x_all[batch, :, :, q].reshape(nsig * bs, tile), fm_all[...].reshape(nsig * bs, half),
                    (((0,), (0,)), ((), ())), preferred_element_type=F32,
                )
                dist2 = None
                for axis in range(3):
                    diff = flipped[q, axis:axis + 1] - pts_ref[batch, axis:axis + 1, lanes]
                    dist2 = diff * diff if dist2 is None else dist2 + diff * diff
                kern = 1.0 / jnp.sqrt(dist2 + 0.5)
                mixed[z, q, :] = (flipped[q, 3:4] * kern * inter).astype(BF16)

            @pl.when(z > 0)
            def _():
                m_copy(z, -1).start()

            @pl.when(z < nrows - 1)
            def _():
                m_copy(z, 1).start()

    def m_arrive(batch):
        for dist in range(1, nrows):
            from_up, from_down = z + dist, z - dist

            @pl.when(jnp.logical_and(from_up >= batch * split, from_up < (batch + 1) * split))
            def _():
                m_copy(from_up, -1).wait_recv()

                @pl.when(z > 0)
                def _():
                    m_copy(from_up, -1).start()

            @pl.when(jnp.logical_and(from_down >= batch * split, from_down < (batch + 1) * split))
            def _():
                m_copy(from_down, 1).wait_recv()

                @pl.when(z < nrows - 1)
                def _():
                    m_copy(from_down, 1).start()

    def potentials(batch):
        for h in range(split):
            cut = slice(h * half, (h + 1) * half)

            def fill_pot(i, carry):
                some = pl.ds(i * 4, 4)
                got = jnp.dot(
                    x_all[batch, some].reshape(4 * bs, npts), mixed[batch * split + h], preferred_element_type=F32
                ) * w_ref[batch:batch + 1, cut]
                pot[batch, some, :, cut] = got.astype(BF16).reshape(4, bs, half)
                return carry
            lax.fori_loop(0, nsig // 4, fill_pot, 0)

    for batch in range(nb):
        for dist in range(1, nrows - 1):
            x_arrive(batch, dist)
            if batch > 0 and dist == 1:
                products(batch - 1)
        if batch + 1 < nb:
            x_begin(batch + 1)
        if batch == 0:
            for k in range(1, nchip):
                p_wait(k).wait_recv()
                p_forward(k).start()
            for k in range(nchip):
                p_pair_wait(k).wait_recv()
        else:
            mix(batch - 1)
        x_arrive(batch, nrows - 1)
        if batch > 1:
            m_arrive(batch - 2)
    products(nb - 1)
    if nb > 1:
        m_arrive(nb - 2)
    mix(nb - 1)
    for batch in range(nb - 1):
        potentials(batch)
    m_arrive(nb - 1)
    potentials(nb - 1)

    total_rows = nblk * rows
    step_rows = min(4 * GROUP, total_rows)
    side = total_rows // 2

    def fill_rhs(dest):
        for t in range(bpd):
            for batch in range(nb):
                rhs[t * bs:(t + 1) * bs, batch * npts:(batch + 1) * npts] = pot[
                    batch, inv_ref[batch, dest * bpd + t]
                ]

    def product(at):
        return lax.dot_general(
            lhs[pl.ds(at, step_rows), :], rhs[...], (((1,), (1,)), ((), ())), preferred_element_type=F32
        )

    def pair_copy(k):
        return remote(pair_send.at[k], pair_recv.at[k], pair_out.at[k], pair_in.at[k], (partner, z))

    def q_copy(k, cut, device):
        at = pl.ds(cut * side, side)
        return remote(q_send.at[k, at], q_recv.at[k, at], q_out.at[k, cut], q_in.at[k, cut], (device, z))

    def s_copy(k, cut, device):
        at = pl.ds(cut * (side // GROUP), side // GROUP)
        return remote(s_send.at[k, at], s_recv.at[k, at], s_out.at[k, cut], s_in.at[k, cut], (device, z))

    def send(k, cut, device):
        q_copy(k, cut, device).start()
        s_copy(k, cut, device).start()

    def arrive(k, cut, device):
        q_copy(k, cut, device).wait_recv()
        s_copy(k, cut, device).wait_recv()

    def encode(k, group, some):
        top = jnp.maximum(jnp.max(jnp.abs(some), axis=0, keepdims=True), TINY)
        s_send[k, group] = jnp.broadcast_to(top * (1.0 / LEVELS), (8, cols))
        q_send[k, pl.ds(pl.multiple_of(group * GROUP, GROUP), GROUP), :] = (
            jnp.round(some * (LEVELS / top)).astype(jnp.int32).astype(jnp.int16)
        )

    def decode(k, group):
        at = pl.ds(pl.multiple_of(group * GROUP, GROUP), GROUP)
        return q_recv[k, at, :].astype(jnp.int32).astype(F32) * s_recv[k, group, 0:1, :]

    def start_pair(k):
        fill_rhs(toward(k) * CORES + (CORES - 1 - core))

        def theirs(i, carry):
            at = pl.multiple_of(i * step_rows, step_rows)
            pair_send[k, pl.ds(at, step_rows), :] = product(at)
            return carry
        lax.fori_loop(0, total_rows // step_rows, theirs, 0)
        pair_copy(k).start()

    def finish_pair(k, keep):
        fill_rhs(toward(k) * CORES + core)
        pair_copy(k).wait_recv()

        def ours(i, carry):
            at = pl.multiple_of(i * step_rows, step_rows)
            value = product(at) + pair_recv[k, pl.ds(at, step_rows), :]
            keep(k, i, at, value)
            return carry
        lax.fori_loop(0, total_rows // step_rows, ours, 0)

    def keep_code(k, i, at, value):
        for g in range(step_rows // GROUP):
            encode(k, i * (step_rows // GROUP) + g, value[g * GROUP:(g + 1) * GROUP])

    def keep_value(k, i, at, value):
        pair_recv[k, pl.ds(at, step_rows), :] = value

    def keep_out(k, i, at, value):
        out_ref[pl.ds(at, step_rows), :] = value

    def groups(cut, step):
        def one(i, carry):
            step(cut * (side // GROUP) + i)
            return carry
        lax.fori_loop(0, side // GROUP, one, 0)

    def add(k, cut):
        def one(group):
            at = pl.ds(pl.multiple_of(group * GROUP, GROUP), GROUP)
            out_ref[at, :] = out_ref[at, :] + decode(k, group)
        groups(cut, one)

    def rows_of(k, group):
        return pair_recv[k, pl.ds(pl.multiple_of(group * GROUP, GROUP), GROUP), :]

    if square:
        flip = {1: peer(1), 2: peer(2)}
        start_pair(3)
        finish_pair(3, keep_code)
        for cut in range(2):
            send(3, cut, flip[cut + 1])
        for k in (1, 2):
            start_pair(k)
            finish_pair(k, keep_value)
            groups(k - 1, lambda group: encode(k, group, rows_of(k, group)))
            send(k, k - 1, flip[k])
        start_pair(0)
        finish_pair(0, keep_out)
        for k in (1, 2):
            cut = 2 - k
            arrive(3, cut, flip[3 - k])
            groups(cut, lambda group: encode(k, group, rows_of(k, group) + decode(3, group)))
            send(k, cut, flip[k])
        for k in (1, 2):
            arrive(k, k - 1, flip[k])
            add(k, k - 1)
        for k in (1, 2):
            arrive(k, 2 - k, flip[k])
            add(k, 2 - k)
        sent = [(3, 0, flip[1]), (3, 1, flip[2])] + [(k, cut, flip[k]) for k in (1, 2) for cut in range(2)]
    else:
        for k in list(range(1, nchip)):
            start_pair(k)
            finish_pair(k, keep_code)
            for cut in range(2):
                send(k, cut, peer(k))
        start_pair(0)
        finish_pair(0, keep_out)
        for k in range(1, nchip):
            for cut in range(2):
                arrive(k, cut, peer(k))
                add(k, cut)
        sent = [(k, cut, peer(k)) for k in range(1, nchip) for cut in range(2)]

    for k, cut, device in sent:
        q_copy(k, cut, device).wait_send()
        s_copy(k, cut, device).wait_send()
    for k in range(nchip):
        p_forward(k).wait_send()
        pair_copy(k).wait_send()
        if k > 0:
            p_copy(k).wait_send()
    for owner in range(nrows):
        @pl.when(z != owner)
        def _():
            fm_copy(owner).wait_send()

        @pl.when(jnp.logical_and(z > 0, owner >= z))
        def _():
            for batch in range(nb):
                for c in range(pieces):
                    x_copy(batch, owner, c, -1).wait_send()
            m_copy(owner, -1).wait_send()

        @pl.when(jnp.logical_and(z < nrows - 1, owner <= z))
        def _():
            for batch in range(nb):
                for c in range(pieces):
                    x_copy(batch, owner, c, 1).wait_send()
            m_copy(owner, 1).wait_send()


def body(ngrid, nrows, density, basis_values, grid_points, grid_weights, screened_blocks):
    nblk, rows, cols = density.shape
    nb, nsig, _, npts = basis_values.shape
    bs = rows * nrows
    nchip = ngrid // CORES
    half = npts // (nrows // nb)
    total_rows = nblk * rows
    hit = screened_blocks[:, None, :] == jnp.arange(nblk, dtype=jnp.int32)[None, :, None]
    slot = jnp.arange(nsig, dtype=jnp.int32)
    inverse = jnp.min(jnp.where(hit, slot, nsig), axis=2).astype(jnp.int32)
    vmem = pl.BlockSpec(memory_space=pltpu.VMEM)
    smem = pl.BlockSpec(memory_space=pltpu.SMEM)
    dma = pltpu.SemaphoreType.DMA
    out = pl.pallas_call(
        functools.partial(kernel, ngrid, nrows),
        out_shape=jax.ShapeDtypeStruct((total_rows, cols), F32),
        in_specs=[smem, smem] + [vmem] * 4,
        out_specs=vmem,
        scratch_shapes=[
            pltpu.VMEM((cols // bs, nblk, rows, bs), BF16),
            pltpu.VMEM((nblk, nblk, rows, bs), BF16),
            pltpu.VMEM((nb, nsig, bs, npts), BF16),
            pltpu.VMEM((nsig * rows, nsig * bs), BF16),
            pltpu.VMEM((nrows, nsig, rows, half), BF16),
            pltpu.VMEM((nsig, bs, half), BF16),
            pltpu.VMEM((nrows, npts, half), BF16),
            pltpu.VMEM((nb, nsig + 1, rows, npts), BF16),
            pltpu.VMEM((nb, nsig + 1, bs, npts), BF16),
            pltpu.VMEM((total_rows, nb * npts), BF16),
            pltpu.VMEM((cols, nb * npts), BF16),
            pltpu.VMEM((nchip, total_rows, cols), F32),
            pltpu.VMEM((nchip, total_rows, cols), F32),
            pltpu.VMEM((nchip, total_rows, cols), jnp.int16),
            pltpu.VMEM((nchip, total_rows, cols), jnp.int16),
            pltpu.VMEM((nchip, total_rows // GROUP, 8, cols), F32),
            pltpu.VMEM((nchip, total_rows // GROUP, 8, cols), F32),
            dma((nchip,)), dma((nchip,)), dma((ngrid,)),
            dma((nb, nrows, 2)), dma((nb, nrows, 2)), dma((nb, nrows, 2)),
            dma((1 + 3 * nb,)),
            dma((nrows,)), dma((nrows,)),
            dma((nrows,)), dma((nrows,)), dma((nrows,)),
            dma((nchip,)), dma((nchip,)),
            dma((nchip, 2)), dma((nchip, 2)), dma((nchip, 2)), dma((nchip, 2)),
        ],
        compiler_params=pltpu.CompilerParams(
            collective_id=0, has_side_effects=True, vmem_limit_bytes=63 * 1024 * 1024
        ),
        name="exchange",
    )(screened_blocks, inverse, density, basis_values, grid_points, grid_weights)
    return out.reshape(nblk, rows, cols)


def solution(mesh):
    placed = (
        P(None, "rows", "grid"),
        P("grid", None, "rows", None),
        P("grid", None, None),
        P("grid", None),
        P("grid", None),
    )
    return jax.shard_map(
        functools.partial(body, mesh.shape["grid"], mesh.shape["rows"]), mesh=mesh, in_specs=placed,
        out_specs=P(None, "rows", "grid"), check_vma=False,
    )
```

time: 208 us -> 210 us (level)
  Pallas kernels: 193 us -> 202 us
  local copies, waits for them, and re-layouts: 11.6 us -> 4.5 us
    pallas_call x1, Pallas kernels: 193 us -> 202 us  [body(): pl.pallas_call(functools.partial(kernel, ngrid, nrows), out_shape=jax.Sha...]
    broadcast_in_dim x2 -> x0, local copies, waits for them, and re-layouts: 3 us -> none  [the longest x1 1.72 us: body(): grid_weights[:, :, None]]
    transpose x1 -> x0, local copies, waits for them, and re-layouts: 2.41 us -> none  [body(): density.reshape(nblk, rows, cols // bs, bs).swapaxes(1, 2)]
    unnamed x3 -> x2, local copies, waits for them, and re-layouts: 6.22 us -> 4.5 us
where the time goes in v2:
time: 210 us; the launch traced here: 208 us
  Pallas kernels  202 us (96%)
  local copies, waits for them, and re-layouts  4.5 us (2%)
    pallas_call x1, Pallas kernels, body(): pl.pallas_call(functools.partial(kernel, ngrid, nrows), out_shape=jax.Sha...  202 us
    unnamed x2, local copies, waits for them, and re-layouts  4.5 us

profile of v2, /device:TPU:2, one launch (start us, length us, event | category | flops | bytes accessed | tf_op | source)
XLA Modules:
  0.0 207.6 jit_solution(16455461619497755938)
XLA Ops:
  0.0 1.4 select_reduce_fusion.inv_ref
  1.4 1.3 copy.7.pts_ref
  2.7 201.7 %exchange.1 = f32[1024,512]{1,0:T(8,128)} custom-call(s32[2,16]{1,0:T(2,128)} %sel_ref.1, s32[2,32]{1,0:T(2,128)} %select_reduce_fusion.inv_ref, bf16[32,32,512]{2,1,0:T(8,128)(2,1)} %p_ref.1, bf16[2,16,32,512]{3,2,1,0:T(8,128)(2,1)} %x_ref.1, f32[2,3,512]{2,1,0:T(4,128)} %copy.7.pts_ref, f32[2,512]{1,0:T(2,128)} %w_ref.1), custom_call_target="tpu_custom_call" | custom-call | tf_op jit(solution)/shard_map/exchange/pallas_call | solution.py:462
  204.4 3.2 %copy.9 = f32[32,32,512]{2,1,0:T(8,128)} copy(f32[32,32,512]{2,1,0:T(8,128)} %bitcast.1) | data formatting | bytes 4194304

commit v3 on v2

--- a/solution.py
+++ b/solution.py
@@ -36,7 +36,7 @@
     bpd = cols // bs
     split = nrows // nb
     half = npts // split
-    pieces = 2
+    pieces = 1
     part = nsig // pieces
 
     def toward(k):
@@ -123,7 +123,8 @@
         slot = source(k) * CORES + (CORES - 1 - core)
         return remote(p_mine, p_slot(slot), p_pair.at[k], p_in.at[slot], (partner, z))
 
-    x_begin(0)
+    for batch in range(nb):
+        x_begin(batch)
     for k in range(1, nchip):
         p_copy(k).start()
     p_forward(0).start()
@@ -227,11 +228,11 @@
             def _():
                 m_copy(z, 1).start()
 
-    def m_arrive(batch):
+    def m_arrive():
         for dist in range(1, nrows):
             from_up, from_down = z + dist, z - dist
 
-            @pl.when(jnp.logical_and(from_up >= batch * split, from_up < (batch + 1) * split))
+            @pl.when(from_up < nrows)
             def _():
                 m_copy(from_up, -1).wait_recv()
 
@@ -239,7 +240,7 @@
                 def _():
                     m_copy(from_up, -1).start()
 
-            @pl.when(jnp.logical_and(from_down >= batch * split, from_down < (batch + 1) * split))
+            @pl.when(from_down >= 0)
             def _():
                 m_copy(from_down, 1).wait_recv()
 
@@ -260,32 +261,22 @@
                 return carry
             lax.fori_loop(0, nsig // 4, fill_pot, 0)
 
-    for batch in range(nb):
-        for dist in range(1, nrows - 1):
+    for dist in range(1, nrows - 1):
+        for batch in range(nb):
             x_arrive(batch, dist)
-            if batch > 0 and dist == 1:
-                products(batch - 1)
-        if batch + 1 < nb:
-            x_begin(batch + 1)
-        if batch == 0:
-            for k in range(1, nchip):
-                p_wait(k).wait_recv()
-                p_forward(k).start()
-            for k in range(nchip):
-                p_pair_wait(k).wait_recv()
-        else:
-            mix(batch - 1)
+    for k in range(1, nchip):
+        p_wait(k).wait_recv()
+        p_forward(k).start()
+    for k in range(nchip):
+        p_pair_wait(k).wait_recv()
+    for batch in range(nb):
         x_arrive(batch, nrows - 1)
-        if batch > 1:
-            m_arrive(batch - 2)
-    products(nb - 1)
-    if nb > 1:
-        m_arrive(nb - 2)
-    mix(nb - 1)
-    for batch in range(nb - 1):
+        products(batch)
+    for batch in range(nb):
+        mix(batch)
+    m_arrive()
+    for batch in range(nb):
         potentials(batch)
-    m_arrive(nb - 1)
-    potentials(nb - 1)
 
     total_rows = nblk * rows
     step_rows = min(4 * GROUP, total_rows)

time: 210 us -> 180 us (0.86)
  Pallas kernels: 202 us -> 172 us
    pallas_call x1, Pallas kernels: 202 us -> 172 us  [body(): pl.pallas_call(functools.partial(kernel, ngrid, nrows), out_shape=jax.Sha...]
where the time goes in v3:
time: 180 us; the launch traced here: 178 us
  Pallas kernels  172 us (96%)
  local copies, waits for them, and re-layouts  4.5 us (2%)
    pallas_call x1, Pallas kernels, body(): pl.pallas_call(functools.partial(kernel, ngrid, nrows), out_shape=jax.Sha...  172 us
    unnamed x2, local copies, waits for them, and re-layouts  4.5 us

profile of v3, /device:TPU:2, one launch (start us, length us, event | category | flops | bytes accessed | tf_op | source)
XLA Modules:
  0.0 178.0 jit_solution(13753661028447385183)
XLA Ops:
  0.0 1.4 select_reduce_fusion.inv_ref
  1.4 1.3 copy.7.pts_ref
  2.7 172.2 %exchange.1 = f32[1024,512]{1,0:T(8,128)} custom-call(s32[2,16]{1,0:T(2,128)} %sel_ref.1, s32[2,32]{1,0:T(2,128)} %select_reduce_fusion.inv_ref, bf16[32,32,512]{2,1,0:T(8,128)(2,1)} %p_ref.1, bf16[2,16,32,512]{3,2,1,0:T(8,128)(2,1)} %x_ref.1, f32[2,3,512]{2,1,0:T(4,128)} %copy.7.pts_ref, f32[2,512]{1,0:T(2,128)} %w_ref.1), custom_call_target="tpu_custom_call" | custom-call | tf_op jit(solution)/shard_map/exchange/pallas_call | solution.py:453
  174.8 3.2 %copy.9 = f32[32,32,512]{2,1,0:T(8,128)} copy(f32[32,32,512]{2,1,0:T(8,128)} %bitcast.1) | data formatting | bytes 4194304
